TPU v7x, 32 devices: a whole 2x2x4 slice. The times are simulated.
32 devices in a mesh: groups: 2 (over y), expert: 4 (over z), tensor: 2 (over x), sub: 2 (over core).
Axes of the slice: x: 2, y: 2, z: 4, core: 2. Of those that a mesh axis runs over, the one named last changes fastest.
Arguments:
- tokens: bfloat16 [48, 7168], P(('groups', 'expert', 'tensor'), 'sub'), parts along dimension 0, may hold values from -6 to 6
- expert_ids: int32 [48, 8], P(('groups', 'expert', 'tensor')), parts along dimension 0, may hold values from 0 to 15, all different within a row; in each aligned block of 3 rows (0 to 2, 3 to 5, ...) at most 2 rows name the same one
- gate_weights: float32 [48, 8], P(('groups', 'expert', 'tensor')), parts along dimension 0, may hold values from 0.1 to 0.6
- gate_proj: bfloat16 [16, 1024, 7168], P('expert', 'tensor', 'sub'), may hold values from -0.0625 to 0.0625
- up_proj: bfloat16 [16, 1024, 7168], P('expert', 'tensor', 'sub'), may hold values from -0.0625 to 0.0625
- down_proj: bfloat16 [16, 1024, 7168], P('expert', 'tensor', 'sub'), may hold values from -0.1875 to 0.1875
Outputs:
- blended: bfloat16 [48, 7168], P(('groups', 'expert', 'tensor'), 'sub'), parts along dimension 0
There are 2 independent parts, one for each index of `groups`. A program takes and returns all parts, laid end to end along the dimension named above; an argument that names none is the same for every part. Nothing has to cross between parts.
Inputs may be any that keep to these rules, and one draw needn't show every extreme that they name: `expert_ids`: each row names 8 different experts. Among the rows of one owner (aligned blocks of 3 rows) no expert is named by more than 2 rows, a bound that some block reaches.
All inputs are finite; a program needn't handle non-finite values.
Results may differ from a plain program's by a relative error of at most 0.02.
Values may be sent and summed in bfloat16 or wider, within the bound.
A program may use at most 128 MiB of HBM per device.

v0:
```python
import functools

import jax
import jax.numpy as jnp
from jax import lax
from jax.experimental import pallas as pl
from jax.experimental.pallas import tpu as pltpu
from jax.sharding import PartitionSpec as P

MESH = pl.DeviceIdType.MESH
LANES = 128
IN_TILES = (8, 8, 12)
TURNED = 2
OUT_TILES = (8, 8, 8, 4)
NT = (((1,), (1,)), ((), ()))


def split(tiles, wanted):
    cuts, at = [], 0
    for want in wanted:
        size = min(want, tiles - at)
        if size > 0:
            cuts.append((at, size))
            at += size
    if at < tiles:
        cuts.append((at, tiles - at))
    return cuts


def pad8(rows):
    return pl.cdiv(rows, 8) * 8


def placed_rows(cuts, owned):
    spots, at = [], 0
    for _, tiles in cuts:
        spots.append((at, pad8(owned * tiles)))
        at += spots[-1][1]
    return spots, at


def kernel(
    sizes,
    tok_ref, ids_ref, gw_ref, gate_ref, up_ref, down_ref, out_ref,
    wg, wu, wd, own_tok, own_ids, own_gw, own_table, message, tok_in, table_in, table, wide, x16,
    own_part, sent_part, got_part, hidden, spread, stage, ret, final,
    turned, w_sem, d_sem, own_sem, in_send, in_recv, table_send, table_recv, part_send, part_recv, ret_send, ret_recv,
):
    expert_count, tensor_count, sub_count = sizes
    peers = expert_count * tensor_count
    local_count, units = gate_ref.shape[0], gate_ref.shape[1]
    owned, features = tok_ref.shape
    tiles = features // LANES
    experts = expert_count * local_count
    out_cuts = split(tiles, OUT_TILES)
    out_spots, _ = placed_rows(out_cuts, owned)
    in_cuts = split(tiles, IN_TILES)
    in_spots, in_rows = placed_rows(in_cuts, owned)
    f32, bf16 = jnp.float32, jnp.bfloat16
    expert_at = lax.axis_index("expert")
    me = expert_at * tensor_count + lax.axis_index("tensor")
    sub = lax.axis_index("sub")

    def peer(k):
        p = lax.rem(me + k, peers)
        return p, {"expert": p // tensor_count, "tensor": lax.rem(p, tensor_count)}

    def core(j):
        return {"sub": lax.rem(sub + j, sub_count)}

    def each_peer(body):
        def step(k, carry):
            body(*peer(k))
            return carry

        lax.fori_loop(1, peers, step, 0, unroll=peers <= 16)

    barrier = pltpu.get_barrier_semaphore()
    each_peer(lambda p, where: pl.semaphore_signal(barrier, inc=1, device_id=where, device_id_type=MESH))
    for j in range(1, sub_count):
        pl.semaphore_signal(barrier, inc=1, device_id=core(j), device_id_type=MESH)

    own = [
        pltpu.make_async_copy(src, dst, own_sem.at[i])
        for i, (src, dst) in enumerate(((tok_ref, own_tok), (ids_ref, own_ids), (gw_ref, own_gw)))
    ]
    for copy in own:
        copy.start()
    loads = [
        [
            [
                pltpu.make_async_copy(
                    src.at[l, :, pl.ds(at * LANES, size * LANES)],
                    dst.at[l, :, pl.ds(at * LANES, size * LANES)],
                    w_sem.at[c, l, i],
                )
                for i, (src, dst) in enumerate(((gate_ref, wg), (up_ref, wu)))
            ]
            for l in range(local_count)
        ]
        for c, (at, size) in enumerate(in_cuts)
    ]
    downs = []
    for c, (at, size) in enumerate(out_cuts):
        columns = pl.ds(at * LANES, size * LANES)
        downs.append(pltpu.make_async_copy(down_ref.at[:, :, columns], wd.at[:, :, columns], d_sem.at[c]))
    for chunk in loads:
        for pair in chunk:
            for load in pair:
                load.start(priority=1)
    for load in downs:
        load.start(priority=1)

    own[0].wait()
    mine = own_tok[...].astype(f32)
    wide[pl.ds(0, in_rows), :] = jnp.zeros((in_rows, LANES), f32)
    for (at, size), (spot, _) in zip(in_cuts, in_spots):
        for t in range(size):
            wide[pl.ds(spot + t, owned, size), :] = mine[:, (at + t) * LANES:(at + t + 1) * LANES]
    message[...] = wide[pl.ds(0, in_rows), :].astype(bf16)
    own[1].wait()
    own[2].wait()
    labels = lax.broadcasted_iota(jnp.int32, (owned, experts), 1)
    weights = jnp.zeros((owned, experts), f32)
    for k in range(own_ids.shape[1]):
        weights = weights + jnp.where(own_ids[:, k:k + 1] == labels, own_gw[:, k:k + 1], 0.0)
    own_table[...] = weights

    pl.semaphore_wait(barrier, peers - 1 + sub_count - 1)

    def send_tokens(c):
        spot, rows = in_spots[c]

        def send(p, where):
            pltpu.make_async_remote_copy(
                src_ref=message.at[pl.ds(spot, rows)], dst_ref=tok_in.at[me, pl.ds(spot, rows)],
                send_sem=in_send.at[c], recv_sem=in_recv.at[c], device_id=where, device_id_type=MESH,
            ).start()

        each_peer(send)

    def send_table(p, where):
        pltpu.make_async_remote_copy(
            src_ref=own_table, dst_ref=table_in.at[me], send_sem=table_send, recv_sem=table_recv,
            device_id=where, device_id_type=MESH,
        ).start()

    for c in range(len(in_cuts)):
        send_tokens(c)
    each_peer(send_table)
    tok_in[me] = message[...]
    table_in[me] = own_table[...]
    spread[...] = jnp.zeros_like(spread)

    for c, (at, size) in enumerate(in_cuts[:TURNED]):
        columns = slice(at * LANES, (at + size) * LANES)
        for l in range(local_count):
            for i, w in enumerate((wg, wu)):
                loads[c][l][i].wait()
                turned[2 * l + i, columns, :] = w[l, :, columns].T

    def exchange(l, j):
        return pltpu.make_async_remote_copy(
            src_ref=sent_part.at[l], dst_ref=got_part.at[l, j - 1],
            send_sem=part_send.at[l, j - 1], recv_sem=part_recv.at[l, j - 1],
            device_id=core(j), device_id_type=MESH,
        )

    def gather(c):
        (at, size), (spot, rows) = in_cuts[c], in_spots[c]
        some = tok_in.at[pl.ds(0, peers - 1), pl.ds(spot, rows)]
        pltpu.make_async_copy(some, some, in_recv.at[c]).wait()
        wide[pl.ds(0, peers * rows), :] = (
            tok_in[:, spot:spot + rows, :].astype(f32).reshape(peers * rows, LANES)
        )
        for t in range(size):
            picked = [wide[pl.ds(r * size + t, peers, rows), :] for r in range(owned)]
            x16[:, (at + t) * LANES:(at + t + 1) * LANES] = jnp.concatenate(picked, axis=0).astype(bf16)

    def first(c, l):
        at, size = in_cuts[c]
        columns = slice(at * LANES, (at + size) * LANES)
        x = x16[:, columns]
        for i, w in enumerate((wg, wu)):
            spot = slice(i * units, (i + 1) * units)
            if c < TURNED:
                part = jnp.dot(x, turned[2 * l + i, columns, :], preferred_element_type=f32)
            else:
                part = lax.dot_general(x, w[l, :, columns], NT, preferred_element_type=f32)
            if c > 0:
                part = own_part[l, :, spot] + part
            own_part[l, :, spot] = part
            if c == len(in_cuts) - 1:
                sent_part[l, :, spot] = part.astype(bf16)
        if c == len(in_cuts) - 1:
            for j in range(1, sub_count):
                exchange(l, j).start()

    def finish(l):
        both = own_part[l]
        for j in range(1, sub_count):
            exchange(l, j).wait()
            both = both + got_part[l, j - 1].astype(f32)
        gate, up = both[:, :units], both[:, units:]
        label = expert_at * local_count + l
        chosen = lax.broadcasted_iota(jnp.int32, table.shape, 1) == label
        weight = jnp.sum(jnp.where(chosen, table[...], 0.0), axis=1, keepdims=True)
        hidden[:, l * units:(l + 1) * units] = (gate / (1.0 + jnp.exp(-gate)) * up * weight).astype(bf16)

    last = len(in_cuts) - 1
    for c in range(last):
        gather(c)
        for l in range(local_count):
            if c >= TURNED:
                for load in loads[c][l]:
                    load.wait()
            first(c, l)
    gather(last)
    some = table_in.at[pl.ds(0, peers - 1)]
    pltpu.make_async_copy(some, some, table_recv).wait()
    for r in range(owned):
        table[r * peers:(r + 1) * peers, :] = table_in[:, r, :]
    for l in range(local_count):
        if last >= TURNED:
            for load in loads[last][l]:
                load.wait()
        first(last, l)
        if l > 0:
            finish(l - 1)
    finish(local_count - 1)

    def give(c):
        spot, rows = out_spots[c]

        def send(p, where):
            pltpu.make_async_remote_copy(
                src_ref=stage.at[p, pl.ds(spot, rows)], dst_ref=ret.at[me, pl.ds(spot, rows)],
                send_sem=ret_send.at[c], recv_sem=ret_recv.at[c], device_id=where, device_id_type=MESH,
            ).start()

        each_peer(send)

    for c, (at, size) in enumerate(out_cuts):
        downs[c].wait()
        w = wd[:, :, at * LANES:(at + size) * LANES].reshape(local_count * units, size * LANES)
        part = jnp.dot(hidden[...], w, preferred_element_type=f32)
        spot, rows = out_spots[c]
        for r in range(owned):
            for t in range(size):
                spread[pl.ds(r * size + t, peers, rows), :] = part[
                    r * peers:(r + 1) * peers, t * LANES:(t + 1) * LANES
                ]
        stage[:, spot:spot + rows, :] = spread[: peers * rows, :].reshape(peers, rows, LANES).astype(bf16)
        give(c)

    for c, (at, size) in enumerate(out_cuts):
        spot, rows = out_spots[c]
        some = ret.at[pl.ds(0, peers - 1), pl.ds(spot, rows)]
        pltpu.make_async_copy(some, some, ret_recv.at[c]).wait()
        ret[me, spot:spot + rows, :] = stage[me, spot:spot + rows, :]
        total = jnp.sum(ret[:, spot:spot + rows, :].astype(f32), axis=0)
        for r in range(owned):
            final[pl.ds(at * 8 + r, size, 8), :] = total[r * size:(r + 1) * size]
        for t in range(at, at + size):
            out_ref[:, t * LANES:(t + 1) * LANES] = final[t * 8:t * 8 + owned, :].astype(bf16)

    for c, (spot, rows) in enumerate(in_spots):
        some = tok_in.at[pl.ds(0, peers - 1), pl.ds(spot, rows)]
        pltpu.make_async_copy(some, some, in_send.at[c]).wait()
    some = table_in.at[pl.ds(0, peers - 1)]
    pltpu.make_async_copy(some, some, table_send).wait()
    for c, (spot, rows) in enumerate(out_spots):
        some = ret.at[pl.ds(0, peers - 1), pl.ds(spot, rows)]
        pltpu.make_async_copy(some, some, ret_send.at[c]).wait()


def solution(mesh):
    expert_count, tensor_count = mesh.shape["expert"], mesh.shape["tensor"]
    sub_count = mesh.shape["sub"]
    peers = expert_count * tensor_count

    def per_device(tokens, expert_ids, gate_weights, gate_proj, up_proj, down_proj):
        owned, features = tokens.shape
        top = expert_ids.shape[1]
        local_count, units = gate_proj.shape[0], gate_proj.shape[1]
        rows = peers * owned
        experts = expert_count * local_count
        others = max(1, sub_count - 1)
        tiles = features // LANES
        in_cuts = split(tiles, IN_TILES)
        in_spots, in_rows = placed_rows(in_cuts, owned)
        turned_tiles = sum(size for _, size in in_cuts[:TURNED])
        out_cuts = split(tiles, OUT_TILES)
        out_spots, out_rows = placed_rows(out_cuts, owned)
        widest = max(size for _, size in out_spots)
        pieces = len(out_cuts)
        bf16, f32 = jnp.bfloat16, jnp.float32
        dma = pltpu.SemaphoreType.DMA
        hbm = pl.BlockSpec(memory_space=pl.ANY)
        return pl.pallas_call(
            functools.partial(kernel, (expert_count, tensor_count, sub_count)),
            out_shape=pltpu.VMEM((owned, features), bf16),
            in_specs=[hbm] * 6,
            out_specs=pl.BlockSpec(memory_space=pltpu.VMEM),
            scratch_shapes=[
                pltpu.VMEM(gate_proj.shape, bf16),
                pltpu.VMEM(up_proj.shape, bf16),
                pltpu.VMEM(down_proj.shape, bf16),
                pltpu.VMEM((owned, features), bf16),
                pltpu.VMEM((owned, top), jnp.int32),
                pltpu.VMEM((owned, top), f32),
                pltpu.VMEM((owned, experts), f32),
                pltpu.VMEM((in_rows, LANES), bf16),
                pltpu.VMEM((peers, in_rows, LANES), bf16),
                pltpu.VMEM((peers, owned, experts), f32),
                pltpu.VMEM((rows, experts), f32),
                pltpu.VMEM((peers * max(size for _, size in in_spots), LANES), f32),
                pltpu.VMEM((rows, features), bf16),
                pltpu.VMEM((local_count, rows, 2 * units), f32),
                pltpu.VMEM((local_count, rows, 2 * units), bf16),
                pltpu.VMEM((local_count, others, rows, 2 * units), bf16),
                pltpu.VMEM((rows, local_count * units), bf16),
                pltpu.VMEM((peers * widest, LANES), f32),
                pltpu.VMEM((peers, out_rows, LANES), bf16),
                pltpu.VMEM((peers, out_rows, LANES), bf16),
                pltpu.VMEM((tiles * 8, LANES), f32),
                pltpu.VMEM((2 * local_count, turned_tiles * LANES, units), bf16),
                dma((len(in_cuts), local_count, 2)),
                dma((pieces,)),
                dma((3,)),
                dma((len(in_cuts),)),
                dma((len(in_cuts),)),
                dma(()),
                dma(()),
                dma((local_count, others)),
                dma((local_count, others)),
                dma((pieces,)),
                dma((pieces,)),
            ],
            compiler_params=pltpu.CompilerParams(
                collective_id=0, has_side_effects=True, vmem_limit_bytes=64000 * 1024
            ),
        )(tokens, expert_ids, gate_weights, gate_proj, up_proj, down_proj)

    placed = (
        P(("groups", "expert", "tensor"), "sub"),
        P(("groups", "expert", "tensor"), None),
        P(("groups", "expert", "tensor"), None),
        P("expert", "tensor", "sub"),
        P("expert", "tensor", "sub"),
        P("expert", "tensor", "sub"),
    )
    return jax.shard_map(
        per_device,
        mesh=mesh,
        in_specs=placed,
        out_specs=P(("groups", "expert", "tensor"), "sub"),
        check_vma=False,
    )
```

profile of v0, /device:TPU:0, one launch (start us, length us, event | category | flops | bytes accessed | tf_op | source)
XLA Modules:
  0.0 27.4 jit_solution(1075711097206854462)
XLA Ops:
  0.0 26.8 %shard_map.64 = bf16[3,3584]{1,0:T(4,128)(2,1)S(1)} custom-call(bf16[3,3584]{1,0:T(4,128)(2,1)} %tok_ref.1, s32[3,8]{1,0:T(4,128)} %ids_ref.1, f32[3,8]{1,0:T(4,128)} %gw_ref.1, bf16[4,512,3584]{2,1,0:T(8,128)(2,1)} %gate_ref.1, bf16[4,512,3584]{2,1,0:T(8,128)(2,1)} %up_ref.1, bf16[4,512,3584]{2,1,0:T(8,128)(2,1)} %down_ref.1), custom_call_target="tpu_custom_call" | custom-call | tf_op jit(solution)/shard_map/pallas_call | solution.py:300
  26.8 0.6 %copy.8 = bf16[3,3584]{1,0:T(4,128)(2,1)} copy(bf16[3,3584]{1,0:T(4,128)(2,1)S(1)} %shard_map.64) | data formatting | bytes 43008
where the time goes:
time: 27.5 us; the launch traced here: 27.4 us
  Pallas kernels  26.8 us (97%)
  local copies, waits for them, and re-layouts  0.61 us (2%)
    pallas_call x1, Pallas kernels, per_device(): pl.pallas_call(functools.partial(kernel, (expert_count, tensor_count, sub...  26.8 us
    unnamed x1, local copies, waits for them, and re-layouts  0.61 us

commit v1 on v0

--- a/solution.py
+++ b/solution.py
@@ -10,8 +10,9 @@
 MESH = pl.DeviceIdType.MESH
 LANES = 128
 IN_TILES = (8, 8, 12)
-TURNED = 2
-OUT_TILES = (8, 8, 8, 4)
+AHEAD = 12
+SHARE = 3
+OUT_TILES = (16, 12)
 NT = (((1,), (1,)), ((), ()))
 
 
@@ -39,12 +40,43 @@
     return spots, at
 
 
+def turn_plan(cuts, local_count):
+    sizes = [size * LANES for _, size in cuts]
+    place, beside = {}, {}
+
+    def of(c):
+        return [(c, l, i) for l in range(local_count) for i in range(2)]
+
+    for c in range(min(2, len(cuts))):
+        for n, job in enumerate(of(c)):
+            place[job] = (c, n * sizes[c])
+    first = [job for c in range(min(2, len(cuts))) for job in of(c)]
+    ahead = max(2 * local_count, AHEAD * local_count // 4)
+    now, later = first[:ahead], first[ahead:]
+    for n, job in enumerate(later):
+        beside.setdefault((0, n * local_count // len(later)), []).append(job)
+    if len(cuts) > 2:
+        rest = of(2)
+        some = min(SHARE * local_count // 4, 2 * local_count * sizes[0] // sizes[2])
+        for n, job in enumerate(rest[:some]):
+            beside.setdefault((1, n * local_count // some), []).append(job)
+            place[job] = (0, n * sizes[2])
+        spot, rest = 0, rest[some:]
+        for l in range(local_count):
+            rest = [job for job in rest if job[1] > l]
+            if rest and spot + sizes[2] <= 2 * local_count * sizes[1]:
+                beside[2, l] = rest[:1]
+                place[rest[0]] = (1, spot)
+                spot, rest = spot + sizes[2], rest[1:]
+    return now, beside, place
+
+
 def kernel(
     sizes,
     tok_ref, ids_ref, gw_ref, gate_ref, up_ref, down_ref, out_ref,
     wg, wu, wd, own_tok, own_ids, own_gw, own_table, message, tok_in, table_in, table, wide, x16,
     own_part, sent_part, got_part, hidden, spread, stage, ret, final,
-    turned, w_sem, d_sem, own_sem, in_send, in_recv, table_send, table_recv, part_send, part_recv, ret_send, ret_recv,
+    turned, early, w_sem, d_sem, own_sem, in_send, in_recv, table_send, table_recv, part_send, part_recv, ret_send, ret_recv,
 ):
     expert_count, tensor_count, sub_count = sizes
     peers = expert_count * tensor_count
@@ -152,12 +184,20 @@
     table_in[me] = own_table[...]
     spread[...] = jnp.zeros_like(spread)
 
-    for c, (at, size) in enumerate(in_cuts[:TURNED]):
-        columns = slice(at * LANES, (at + size) * LANES)
-        for l in range(local_count):
-            for i, w in enumerate((wg, wu)):
-                loads[c][l][i].wait()
-                turned[2 * l + i, columns, :] = w[l, :, columns].T
+    turn_now, turn_beside, turned_at = turn_plan(in_cuts, local_count)
+
+    def turned_unit(job):
+        room, row = turned_at[job]
+        return turned.at[room, pl.ds(row, in_cuts[job[0]][1] * LANES)]
+
+    def turn(job):
+        c, l, i = job
+        at, size = in_cuts[c]
+        turned_unit(job)[...] = (wg, wu)[i][l, :, at * LANES:(at + size) * LANES].T
+
+    for job in turn_now:
+        loads[job[0]][job[1]][job[2]].wait()
+        turn(job)
 
     def exchange(l, j):
         return pltpu.make_async_remote_copy(
@@ -177,14 +217,14 @@
             picked = [wide[pl.ds(r * size + t, peers, rows), :] for r in range(owned)]
             x16[:, (at + t) * LANES:(at + t + 1) * LANES] = jnp.concatenate(picked, axis=0).astype(bf16)
 
-    def first(c, l):
+    def first(c, l, half):
         at, size = in_cuts[c]
         columns = slice(at * LANES, (at + size) * LANES)
         x = x16[:, columns]
-        for i, w in enumerate((wg, wu)):
+        for i, w in ((half, (wg, wu)[half]),):
             spot = slice(i * units, (i + 1) * units)
-            if c < TURNED:
-                part = jnp.dot(x, turned[2 * l + i, columns, :], preferred_element_type=f32)
+            if (c, l, i) in turned_at:
+                part = jnp.dot(x, turned_unit((c, l, i))[...], preferred_element_type=f32)
             else:
                 part = lax.dot_general(x, w[l, :, columns], NT, preferred_element_type=f32)
             if c > 0:
@@ -192,7 +232,7 @@
             own_part[l, :, spot] = part
             if c == len(in_cuts) - 1:
                 sent_part[l, :, spot] = part.astype(bf16)
-        if c == len(in_cuts) - 1:
+        if c == len(in_cuts) - 1 and half == 1:
             for j in range(1, sub_count):
                 exchange(l, j).start()
 
@@ -208,26 +248,39 @@
         hidden[:, l * units:(l + 1) * units] = (gate / (1.0 + jnp.exp(-gate)) * up * weight).astype(bf16)
 
     last = len(in_cuts) - 1
+
+    def ready(c, l):
+        for i in range(2):
+            if (c, l, i) not in turned_at:
+                loads[c][l][i].wait()
+        for job in turn_beside.get((c, l), ()):
+            loads[job[0]][job[1]][job[2]].wait()
+
+    def work(c, l):
+        jobs = turn_beside.get((c, l), ())
+        first(c, l, 0)
+        for job in jobs:
+            turn(job)
+        first(c, l, 1)
+
     for c in range(last):
         gather(c)
         for l in range(local_count):
-            if c >= TURNED:
-                for load in loads[c][l]:
-                    load.wait()
-            first(c, l)
+            ready(c, l)
+        for l in range(local_count):
+            work(c, l)
     gather(last)
     some = table_in.at[pl.ds(0, peers - 1)]
     pltpu.make_async_copy(some, some, table_recv).wait()
     for r in range(owned):
         table[r * peers:(r + 1) * peers, :] = table_in[:, r, :]
     for l in range(local_count):
-        if last >= TURNED:
-            for load in loads[last][l]:
-                load.wait()
-        first(last, l)
-        if l > 0:
-            finish(l - 1)
-    finish(local_count - 1)
+        ready(last, l)
+        work(last, l)
+        if l > 1:
+            finish(l - 2)
+    if local_count > 1:
+        finish(local_count - 2)
 
     def give(c):
         spot, rows = out_spots[c]
@@ -242,8 +295,19 @@
 
     for c, (at, size) in enumerate(out_cuts):
         downs[c].wait()
-        w = wd[:, :, at * LANES:(at + size) * LANES].reshape(local_count * units, size * LANES)
-        part = jnp.dot(hidden[...], w, preferred_element_type=f32)
+        columns = slice(at * LANES, (at + size) * LANES)
+        if c == 0:
+            done = (local_count - 1) * units
+            if local_count > 1:
+                w = wd[: local_count - 1, :, columns].reshape(done, size * LANES)
+                early[...] = jnp.dot(hidden[:, :done], w, preferred_element_type=f32)
+            finish(local_count - 1)
+            part = jnp.dot(hidden[:, done:], wd[local_count - 1, :, columns], preferred_element_type=f32)
+            if local_count > 1:
+                part = early[...] + part
+        else:
+            w = wd[:, :, columns].reshape(local_count * units, size * LANES)
+            part = jnp.dot(hidden[...], w, preferred_element_type=f32)
         spot, rows = out_spots[c]
         for r in range(owned):
             for t in range(size):
@@ -289,7 +353,7 @@
         tiles = features // LANES
         in_cuts = split(tiles, IN_TILES)
         in_spots, in_rows = placed_rows(in_cuts, owned)
-        turned_tiles = sum(size for _, size in in_cuts[:TURNED])
+        turned_tiles = max(size for _, size in in_cuts[:2])
         out_cuts = split(tiles, OUT_TILES)
         out_spots, out_rows = placed_rows(out_cuts, owned)
         widest = max(size for _, size in out_spots)
@@ -324,7 +388,8 @@
                 pltpu.VMEM((peers, out_rows, LANES), bf16),
                 pltpu.VMEM((peers, out_rows, LANES), bf16),
                 pltpu.VMEM((tiles * 8, LANES), f32),
-                pltpu.VMEM((2 * local_count, turned_tiles * LANES, units), bf16),
+                pltpu.VMEM((2, 2 * local_count * turned_tiles * LANES, units), bf16),
+                pltpu.VMEM((rows, out_cuts[0][1] * LANES), f32),
                 dma((len(in_cuts), local_count, 2)),
                 dma((pieces,)),
                 dma((3,)),

time: 27.5 us -> 25.3 us (0.920)
  Pallas kernels: 26.8 us -> 24.5 us
    pallas_call x1, Pallas kernels: 26.8 us -> 24.5 us  [per_device(): pl.pallas_call(functools.partial(kernel, (expert_count, tensor_count, sub...]
where the time goes in v1:
time: 25.3 us; the launch traced here: 25.1 us
  Pallas kernels  24.5 us (97%)
  local copies, waits for them, and re-layouts  0.61 us (2%)
    pallas_call x1, Pallas kernels, per_device(): pl.pallas_call(functools.partial(kernel, (expert_count, tensor_count, sub...  24.5 us
    unnamed x1, local copies, waits for them, and re-layouts  0.61 us

profile of v1, /device:TPU:0, one launch (start us, length us, event | category | flops | bytes accessed | tf_op | source)
XLA Modules:
  0.0 25.1 jit_solution(6653444154265036817)
XLA Ops:
  0.0 24.5 %shard_map.64 = bf16[3,3584]{1,0:T(4,128)(2,1)S(1)} custom-call(bf16[3,3584]{1,0:T(4,128)(2,1)} %tok_ref.1, s32[3,8]{1,0:T(4,128)} %ids_ref.1, f32[3,8]{1,0:T(4,128)} %gw_ref.1, bf16[4,512,3584]{2,1,0:T(8,128)(2,1)} %gate_ref.1, bf16[4,512,3584]{2,1,0:T(8,128)(2,1)} %up_ref.1, bf16[4,512,3584]{2,1,0:T(8,128)(2,1)} %down_ref.1), custom_call_target="tpu_custom_call" | custom-call | tf_op jit(solution)/shard_map/pallas_call | solution.py:364
  24.5 0.6 %copy.8 = bf16[3,3584]{1,0:T(4,128)(2,1)} copy(bf16[3,3584]{1,0:T(4,128)(2,1)S(1)} %shard_map.64) | data formatting | bytes 43008

commit v2 on v1

--- a/solution.py
+++ b/solution.py
@@ -11,8 +11,8 @@
 LANES = 128
 IN_TILES = (8, 8, 12)
 AHEAD = 12
-SHARE = 3
-OUT_TILES = (16, 12)
+SHARE = 2
+OUT_TILES = (12, 16)
 NT = (((1,), (1,)), ((), ()))
 
 
@@ -76,7 +76,7 @@
     tok_ref, ids_ref, gw_ref, gate_ref, up_ref, down_ref, out_ref,
     wg, wu, wd, own_tok, own_ids, own_gw, own_table, message, tok_in, table_in, table, wide, x16,
     own_part, sent_part, got_part, hidden, spread, stage, ret, final,
-    turned, early, w_sem, d_sem, own_sem, in_send, in_recv, table_send, table_recv, part_send, part_recv, ret_send, ret_recv,
+    turned, early, marks, w_sem, d_sem, own_sem, in_send, in_recv, table_send, table_recv, part_send, part_recv, ret_send, ret_recv,
 ):
     expert_count, tensor_count, sub_count = sizes
     peers = expert_count * tensor_count
@@ -177,9 +177,9 @@
             device_id=where, device_id_type=MESH,
         ).start()
 
+    each_peer(send_table)
     for c in range(len(in_cuts)):
         send_tokens(c)
-    each_peer(send_table)
     tok_in[me] = message[...]
     table_in[me] = own_table[...]
     spread[...] = jnp.zeros_like(spread)
@@ -214,13 +214,15 @@
             tok_in[:, spot:spot + rows, :].astype(f32).reshape(peers * rows, LANES)
         )
         for t in range(size):
-            picked = [wide[pl.ds(r * size + t, peers, rows), :] for r in range(owned)]
-            x16[:, (at + t) * LANES:(at + t + 1) * LANES] = jnp.concatenate(picked, axis=0).astype(bf16)
+            one, two, three = [wide[pl.ds(r * size + t, peers, rows), :] for r in range(owned)]
+            for l in range(local_count):
+                picked = [jnp.where(marks[l, 0] != 0.0, one, two), jnp.where(marks[l, 1] != 0.0, three, two)]
+                x16[l, :, (at + t) * LANES:(at + t + 1) * LANES] = jnp.concatenate(picked, axis=0).astype(bf16)
 
     def first(c, l, half):
         at, size = in_cuts[c]
         columns = slice(at * LANES, (at + size) * LANES)
-        x = x16[:, columns]
+        x = x16[l, :, columns]
         for i, w in ((half, (wg, wu)[half]),):
             spot = slice(i * units, (i + 1) * units)
             if (c, l, i) in turned_at:
@@ -242,10 +244,34 @@
             exchange(l, j).wait()
             both = both + got_part[l, j - 1].astype(f32)
         gate, up = both[:, :units], both[:, units:]
-        label = expert_at * local_count + l
-        chosen = lax.broadcasted_iota(jnp.int32, table.shape, 1) == label
-        weight = jnp.sum(jnp.where(chosen, table[...], 0.0), axis=1, keepdims=True)
-        hidden[:, l * units:(l + 1) * units] = (gate / (1.0 + jnp.exp(-gate)) * up * weight).astype(bf16)
+        gated = gate / (1.0 + jnp.exp(-gate)) * up
+        first_in, third_in, weight_a, weight_b = [
+            jnp.concatenate([marks[l, i]] * (units // LANES), axis=1) for i in range(4)
+        ]
+        a, b = gated[:peers] * weight_a, gated[peers:] * weight_b
+        back = [
+            jnp.where(first_in != 0.0, a, 0.0),
+            jnp.where(first_in != 0.0, 0.0, a) + jnp.where(third_in != 0.0, 0.0, b),
+            jnp.where(third_in != 0.0, b, 0.0),
+        ]
+        hidden[:, l * units:(l + 1) * units] = jnp.concatenate(back, axis=0).astype(bf16)
+
+    def mark():
+        some = table_in.at[pl.ds(0, peers - 1)]
+        pltpu.make_async_copy(some, some, table_recv).wait()
+        for r in range(owned):
+            table[r * peers:(r + 1) * peers, :] = table_in[:, r, :]
+        labels = lax.broadcasted_iota(jnp.int32, (peers, experts), 1)
+        for l in range(local_count):
+            chosen = labels == expert_at * local_count + l
+            one, two, three = [
+                jnp.sum(jnp.where(chosen, table[r * peers:(r + 1) * peers, :], 0.0), axis=1, keepdims=True)
+                for r in range(owned)
+            ]
+            weight_a = jnp.where(one != 0.0, one, two)
+            weight_b = jnp.where(three != 0.0, three, jnp.where(one != 0.0, two, 0.0))
+            for i, column in enumerate((one, three, weight_a, weight_b)):
+                marks[l, i] = jnp.broadcast_to(column, (peers, LANES))
 
     last = len(in_cuts) - 1
 
@@ -263,6 +289,7 @@
             turn(job)
         first(c, l, 1)
 
+    mark()
     for c in range(last):
         gather(c)
         for l in range(local_count):
@@ -270,10 +297,6 @@
         for l in range(local_count):
             work(c, l)
     gather(last)
-    some = table_in.at[pl.ds(0, peers - 1)]
-    pltpu.make_async_copy(some, some, table_recv).wait()
-    for r in range(owned):
-        table[r * peers:(r + 1) * peers, :] = table_in[:, r, :]
     for l in range(local_count):
         ready(last, l)
         work(last, l)
@@ -379,10 +402,10 @@
                 pltpu.VMEM((peers, owned, experts), f32),
                 pltpu.VMEM((rows, experts), f32),
                 pltpu.VMEM((peers * max(size for _, size in in_spots), LANES), f32),
-                pltpu.VMEM((rows, features), bf16),
-                pltpu.VMEM((local_count, rows, 2 * units), f32),
-                pltpu.VMEM((local_count, rows, 2 * units), bf16),
-                pltpu.VMEM((local_count, others, rows, 2 * units), bf16),
+                pltpu.VMEM((local_count, 2 * peers, features), bf16),
+                pltpu.VMEM((local_count, 2 * peers, 2 * units), f32),
+                pltpu.VMEM((local_count, 2 * peers, 2 * units), bf16),
+                pltpu.VMEM((local_count, others, 2 * peers, 2 * units), bf16),
                 pltpu.VMEM((rows, local_count * units), bf16),
                 pltpu.VMEM((peers * widest, LANES), f32),
                 pltpu.VMEM((peers, out_rows, LANES), bf16),
@@ -390,6 +413,7 @@
                 pltpu.VMEM((tiles * 8, LANES), f32),
                 pltpu.VMEM((2, 2 * local_count * turned_tiles * LANES, units), bf16),
                 pltpu.VMEM((rows, out_cuts[0][1] * LANES), f32),
+                pltpu.VMEM((local_count, 4, peers, LANES), f32),
                 dma((len(in_cuts), local_count, 2)),
                 dma((pieces,)),
                 dma((3,)),

time: 25.3 us -> 24.4 us (0.964)
  Pallas kernels: 24.5 us -> 23.6 us
    pallas_call x1, Pallas kernels: 24.5 us -> 23.6 us  [per_device(): pl.pallas_call(functools.partial(kernel, (expert_count, tensor_count, sub...]
where the time goes in v2:
time: 24.4 us; the launch traced here: 24.2 us
  Pallas kernels  23.6 us (97%)
  local copies, waits for them, and re-layouts  0.61 us (2%)
    pallas_call x1, Pallas kernels, per_device(): pl.pallas_call(functools.partial(kernel, (expert_count, tensor_count, sub...  23.6 us
    unnamed x1, local copies, waits for them, and re-layouts  0.61 us

profile of v2, /device:TPU:0, one launch (start us, length us, event | category | flops | bytes accessed | tf_op | source)
XLA Modules:
  0.0 24.2 jit_solution(12448610677114277445)
XLA Ops:
  0.0 23.6 %shard_map.64 = bf16[3,3584]{1,0:T(4,128)(2,1)S(1)} custom-call(bf16[3,3584]{1,0:T(4,128)(2,1)} %tok_ref.1, s32[3,8]{1,0:T(4,128)} %ids_ref.1, f32[3,8]{1,0:T(4,128)} %gw_ref.1, bf16[4,512,3584]{2,1,0:T(8,128)(2,1)} %gate_ref.1, bf16[4,512,3584]{2,1,0:T(8,128)(2,1)} %up_ref.1, bf16[4,512,3584]{2,1,0:T(8,128)(2,1)} %down_ref.1), custom_call_target="tpu_custom_call" | custom-call | tf_op jit(solution)/shard_map/pallas_call | solution.py:387
  23.6 0.6 %copy.8 = bf16[3,3584]{1,0:T(4,128)(2,1)} copy(bf16[3,3584]{1,0:T(4,128)(2,1)S(1)} %shard_map.64) | data formatting | bytes 43008

commit v3 on v2

--- a/solution.py
+++ b/solution.py
@@ -245,16 +245,8 @@
             both = both + got_part[l, j - 1].astype(f32)
         gate, up = both[:, :units], both[:, units:]
         gated = gate / (1.0 + jnp.exp(-gate)) * up
-        first_in, third_in, weight_a, weight_b = [
-            jnp.concatenate([marks[l, i]] * (units // LANES), axis=1) for i in range(4)
-        ]
-        a, b = gated[:peers] * weight_a, gated[peers:] * weight_b
-        back = [
-            jnp.where(first_in != 0.0, a, 0.0),
-            jnp.where(first_in != 0.0, 0.0, a) + jnp.where(third_in != 0.0, 0.0, b),
-            jnp.where(third_in != 0.0, b, 0.0),
-        ]
-        hidden[:, l * units:(l + 1) * units] = jnp.concatenate(back, axis=0).astype(bf16)
+        weight = jnp.concatenate([jnp.concatenate([marks[l, i]] * (units // LANES), axis=1) for i in (2, 3)], axis=0)
+        hidden[l] = (gated * weight).astype(bf16)
 
     def mark():
         some = table_in.at[pl.ds(0, peers - 1)]
@@ -319,24 +311,27 @@
     for c, (at, size) in enumerate(out_cuts):
         downs[c].wait()
         columns = slice(at * LANES, (at + size) * LANES)
-        if c == 0:
-            done = (local_count - 1) * units
-            if local_count > 1:
-                w = wd[: local_count - 1, :, columns].reshape(done, size * LANES)
-                early[...] = jnp.dot(hidden[:, :done], w, preferred_element_type=f32)
-            finish(local_count - 1)
-            part = jnp.dot(hidden[:, done:], wd[local_count - 1, :, columns], preferred_element_type=f32)
-            if local_count > 1:
-                part = early[...] + part
-        else:
-            w = wd[:, :, columns].reshape(local_count * units, size * LANES)
-            part = jnp.dot(hidden[...], w, preferred_element_type=f32)
+        sums = None
+        for l in range(local_count):
+            if c == 0 and l == local_count - 1:
+                if l > 0:
+                    early[...] = jnp.concatenate(sums, axis=0)
+                finish(l)
+                if l > 0:
+                    sums = [early[r * peers:(r + 1) * peers, :] for r in range(owned)]
+            part = jnp.dot(hidden[l], wd[l, :, columns], preferred_element_type=f32)
+            a, b = part[:peers], part[peers:]
+            is_one, is_three = [jnp.concatenate([marks[l, i]] * size, axis=1) != 0.0 for i in range(2)]
+            back = [
+                jnp.where(is_one, a, 0.0),
+                jnp.where(is_one, 0.0, a) + jnp.where(is_three, 0.0, b),
+                jnp.where(is_three, b, 0.0),
+            ]
+            sums = back if sums is None else [have + more for have, more in zip(sums, back)]
         spot, rows = out_spots[c]
         for r in range(owned):
             for t in range(size):
-                spread[pl.ds(r * size + t, peers, rows), :] = part[
-                    r * peers:(r + 1) * peers, t * LANES:(t + 1) * LANES
-                ]
+                spread[pl.ds(r * size + t, peers, rows), :] = sums[r][:, t * LANES:(t + 1) * LANES]
         stage[:, spot:spot + rows, :] = spread[: peers * rows, :].reshape(peers, rows, LANES).astype(bf16)
         give(c)
 
@@ -406,7 +401,7 @@
                 pltpu.VMEM((local_count, 2 * peers, 2 * units), f32),
                 pltpu.VMEM((local_count, 2 * peers, 2 * units), bf16),
                 pltpu.VMEM((local_count, others, 2 * peers, 2 * units), bf16),
-                pltpu.VMEM((rows, local_count * units), bf16),
+                pltpu.VMEM((local_count, 2 * peers, units), bf16),
                 pltpu.VMEM((peers * widest, LANES), f32),
                 pltpu.VMEM((peers, out_rows, LANES), bf16),
                 pltpu.VMEM((peers, out_rows, LANES), bf16),

time: 24.4 us -> 24.1 us (0.988)
  Pallas kernels: 23.6 us -> 23.3 us
    pallas_call x1, Pallas kernels: 23.6 us -> 23.3 us  [per_device(): pl.pallas_call(functools.partial(kernel, (expert_count, tensor_count, sub...]
where the time goes in v3:
time: 24.1 us; the launch traced here: 23.9 us
  Pallas kernels  23.3 us (97%)
  local copies, waits for them, and re-layouts  0.61 us (3%)
    pallas_call x1, Pallas kernels, per_device(): pl.pallas_call(functools.partial(kernel, (expert_count, tensor_count, sub...  23.3 us
    unnamed x1, local copies, waits for them, and re-layouts  0.61 us

profile of v3, /device:TPU:0, one launch (start us, length us, event | category | flops | bytes accessed | tf_op | source)
XLA Modules:
  0.0 23.9 jit_solution(13874837550096126908)
XLA Ops:
  0.0 23.3 %shard_map.64 = bf16[3,3584]{1,0:T(4,128)(2,1)S(1)} custom-call(bf16[3,3584]{1,0:T(4,128)(2,1)} %tok_ref.1, s32[3,8]{1,0:T(4,128)} %ids_ref.1, f32[3,8]{1,0:T(4,128)} %gw_ref.1, bf16[4,512,3584]{2,1,0:T(8,128)(2,1)} %gate_ref.1, bf16[4,512,3584]{2,1,0:T(8,128)(2,1)} %up_ref.1, bf16[4,512,3584]{2,1,0:T(8,128)(2,1)} %down_ref.1), custom_call_target="tpu_custom_call" | custom-call | tf_op jit(solution)/shard_map/pallas_call | solution.py:382
  23.3 0.6 %copy.8 = bf16[3,3584]{1,0:T(4,128)(2,1)} copy(bf16[3,3584]{1,0:T(4,128)(2,1)S(1)} %shard_map.64) | data formatting | bytes 43008
